TPU v7x, 32 devices: a whole 2x2x4 slice. The times are simulated.
32 devices in a mesh: role: 4 (over z), dp: 2 (over x), tp: 4 (over y, core).
Axes of the slice: x: 2, y: 2, z: 4, core: 2. Of those that a mesh axis runs over, the one named last changes fastest.
Arguments:
- activations: bfloat16 [2048, 8192], P(('role', 'dp'), 'tp'), may hold values from -6 to 6
- cotangent: bfloat16 [2048, 14336], P(('role', 'dp'), 'tp'), may hold values from -6 to 6
- block_keep: int32 [8], P(('role', 'dp')), may hold values 0 or 1
- input_factor: float32 [64, 8192], P(('role', 'dp'), 'tp'), may hold values from -0.5 to 0.5
- input_mean: float32 [64, 8192], P(('role', 'dp'), 'tp'), may hold values from -6 to 6
- input_square: float32 [64, 8192], P(('role', 'dp'), 'tp'), may hold values from 0.5 to 4
- output_factor: float32 [64, 14336], P(('role', 'dp'), 'tp'), may hold values from -0.3125 to 0.3125
- output_mean: float32 [64, 14336], P(('role', 'dp'), 'tp'), may hold values from -6 to 6
- output_square: float32 [64, 14336], P(('role', 'dp'), 'tp'), may hold values from 0.5 to 4
- frozen_base_rows: bfloat16 [14336, 8192], P(('dp', 'tp')), may hold values from -0.0625 to 0.0625
- prompts: bfloat16 [1024, 8192], P(('role', 'dp', 'tp')), may hold values from -6 to 6
Outputs:
- updated_input: float32 [64, 8192], P(('role', 'dp'), 'tp')
- updated_output: float32 [64, 14336], P(('role', 'dp'), 'tp')
- mean_input: float32 [64, 8192], P(('role', 'dp'), 'tp')
- mean_output: float32 [64, 14336], P(('role', 'dp'), 'tp')
- square_input: float32 [64, 8192], P(('role', 'dp'), 'tp')
- square_output: float32 [64, 14336], P(('role', 'dp'), 'tp')
- merged_weight_rows: bfloat16 [14336, 8192], P(('dp', 'tp'))
- projected: bfloat16 [14336, 1024], P(('dp', 'tp'), 'role')
All inputs are finite; a program needn't handle non-finite values. No bound on the sum of `block_keep` on one device may be relied on, other than what follows from the above.
Results may differ from a plain program's by a relative error of at most 0.006.
Values may be sent and summed in bfloat16 or wider, within the bound.
No kernel may reach another device: no remote copies, remote signals or barrier semaphores. Data moves between devices by JAX's collectives and lax.ppermute only.
A program may use at most 128 MiB of HBM per device.

v0:
```python
import jax
import jax.numpy as jnp
from jax import lax
from jax.sharding import PartitionSpec as P

ROLLOUT_TOKENS = 256


adapter_scale = 2.0
learn_rate = 0.004
beta_one = 0.9
beta_two = 0.95
epsilon = 1e-08
first_fix = 1.0 - 0.9**20
second_fix = 1.0 - 0.95**20


def adam_update(factor, moment, square, gradient):
    moment_new = beta_one * moment + (1.0 - beta_one) * gradient
    square_new = beta_two * square + (1.0 - beta_two) * gradient * gradient
    factor_new = factor - learn_rate * (moment_new / first_fix) / (
        jnp.sqrt(square_new / second_fix) + epsilon
    )
    return (factor_new, moment_new, square_new)


def masked(values, block_keep):
    blocks = block_keep.shape[0]
    reshaped_rows = values.reshape(blocks, values.shape[0] // blocks, values.shape[1])
    weighted = reshaped_rows * block_keep.astype(jnp.float32)[:, None, None]
    return weighted.reshape(values.shape).astype(jnp.bfloat16)


def contract_rows(left, right):
    return lax.dot_general(
        left, right, (((0,), (0,)), ((), ())), preferred_element_type=jnp.float32
    )


def contract_cols(left, right):
    return lax.dot_general(
        left, right, (((1,), (1,)), ((), ())), preferred_element_type=jnp.float32
    )


def body(
    activations,
    cotangent,
    block_keep,
    input_factor,
    input_mean,
    input_square,
    output_factor,
    output_mean,
    output_square,
    frozen_base_rows,
    prompts,
):
    input_rows, output_rows = (
        lax.all_gather(input_factor.astype(jnp.bfloat16), ("role", "dp"), axis=0, tiled=True),
        lax.all_gather(output_factor.astype(jnp.bfloat16), ("role", "dp"), axis=0, tiled=True),
    )
    low_input = jnp.dot(activations, input_rows.T, preferred_element_type=jnp.float32)
    low_grad = jnp.dot(cotangent, output_rows.T, preferred_element_type=jnp.float32)
    low_input, low_grad = lax.psum((low_input, low_grad), "tp")
    input_kept = masked(low_input, block_keep)
    grad_kept = masked(low_grad, block_keep)
    input_part = contract_rows(grad_kept, activations)
    output_part = contract_rows(input_kept, cotangent)
    group_input, group_output = (
        lax.psum_scatter(input_part, "role", scatter_dimension=0, tiled=True),
        lax.psum_scatter(output_part, "role", scatter_dimension=0, tiled=True),
    )
    input_sum, output_sum = (
        lax.psum_scatter(group_input, "dp", scatter_dimension=0, tiled=True),
        lax.psum_scatter(group_output, "dp", scatter_dimension=0, tiled=True),
    )
    adapter_factor_scale = adapter_scale / ROLLOUT_TOKENS
    input_new, input_moment, input_second = adam_update(
        input_factor, input_mean, input_square, input_sum * adapter_factor_scale
    )
    output_new, output_moment, output_second = adam_update(
        output_factor, output_mean, output_square, output_sum * adapter_factor_scale
    )
    input_send = input_new.astype(jnp.bfloat16)
    output_send = output_new.astype(jnp.bfloat16)
    input_cols, output_cols = (
        lax.all_gather(input_send, ("role", "dp"), axis=0, tiled=True),
        lax.all_gather(output_send, ("role", "dp"), axis=0, tiled=True),
    )
    input_whole, output_whole = (
        lax.all_gather(input_cols, "tp", axis=1, tiled=True),
        lax.all_gather(output_cols, "tp", axis=1, tiled=True),
    )
    rows_here = frozen_base_rows.shape[0]
    row_block = lax.axis_index("dp") * lax.axis_size("tp") + lax.axis_index("tp")
    output_slice = lax.dynamic_slice_in_dim(output_whole, row_block * rows_here, rows_here, 1)
    adapter_delta_rows = contract_rows(output_slice, input_whole)
    merged_weight_rows = (
        frozen_base_rows.astype(jnp.float32) + adapter_scale * adapter_delta_rows
    ).astype(jnp.bfloat16)
    group_prompts = lax.all_gather(prompts, ("dp", "tp"), axis=0, tiled=True)
    projected = contract_cols(merged_weight_rows, group_prompts)
    return (
        input_new,
        output_new,
        input_moment,
        output_moment,
        input_second,
        output_second,
        merged_weight_rows,
        projected.astype(jnp.bfloat16),
    )


def solution(mesh):
    placed = (
        P(("role", "dp"), "tp"),
        P(("role", "dp"), "tp"),
        P(("role", "dp")),
        P(("role", "dp"), "tp"),
        P(("role", "dp"), "tp"),
        P(("role", "dp"), "tp"),
        P(("role", "dp"), "tp"),
        P(("role", "dp"), "tp"),
        P(("role", "dp"), "tp"),
        P(("dp", "tp"), None),
        P(("role", "dp", "tp"), None),
    )
    return jax.shard_map(
        body,
        mesh=mesh,
        in_specs=placed,
        out_specs=(
            P(("role", "dp"), "tp"),
            P(("role", "dp"), "tp"),
            P(("role", "dp"), "tp"),
            P(("role", "dp"), "tp"),
            P(("role", "dp"), "tp"),
            P(("role", "dp"), "tp"),
            P(("dp", "tp"), None),
            P(("dp", "tp"), "role"),
        ),
        check_vma=False,
    )
```

profile of v0, /device:TPU:0, one launch (start us, length us, event | category | flops | bytes accessed | tf_op | source)
XLA Modules:
  0.0 323.7 jit_solution(6785489352362475291)
XLA Ops:
  7.2 0.0 copy-start
  7.2 0.0 copy-start.2
  7.2 0.0 all-reduce.3.cloned.1.call-start
  7.2 1.1 convert_element_type.31
  8.3 32.9 %all_gather.21 = bf16[64,3584]{1,0:T(8,128)(2,1)S(1)} all-gather(bf16[8,3584]{1,0:T(8,128)(2,1)S(1)} %convert_element_type.31), channel_id=1, replica_groups=mesh['role'=4,'dp'=2,'tp'=4] {'role','dp'}, dimensions={0}, use_global_device_ids=true | all-gather | bytes 516096 | tf_op jit(solution)/shard_map/all_gather | solution.py:61
  41.2 0.8 convert_element_type.34
  42.0 30.7 %all_gather.22 = bf16[64,2048]{1,0:T(8,128)(2,1)S(1)} all-gather(bf16[8,2048]{1,0:T(8,128)(2,1)S(1)} %convert_element_type.34), channel_id=1, replica_groups=mesh['role'=4,'dp'=2,'tp'=4] {'role','dp'}, dimensions={0}, use_global_device_ids=true | all-gather | bytes 294912 | tf_op jit(solution)/shard_map/all_gather | solution.py:60
  72.7 0.0 copy-done
  72.7 1.3 fusion.8
  74.0 0.0 copy-start.4
  74.0 0.0 copy-start.7
  74.0 0.0 copy-start.8
  74.0 2.3 fusion.9
  76.4 0.0 copy-start.3
  76.4 0.0 copy-start.5
  76.4 0.0 copy-start.6
  76.4 0.0 all-reduce.3.cloned.1.call-update
  76.4 0.0 reduce-scatter.5.cloned.1.call-start
  77.2 32.8 %all-reduce.3.cloned.1.call-done = (f32[256,64]{1,0:T(8,128)}, f32[256,64]{1,0:T(8,128)}) async-done(((f32[256,64]{1,0:T(8,128)}, f32[256,64]{1,0:T(8,128)}), (f32[256,64]{1,0:T(8,128)}, f32[256,64]{1,0:T(8,128)})) %all-reduce.3.cloned.1.call-update) | async-done | bytes 131088 | tf_op jit(solution)/shard_map/psum | solution.py:65
  110.0 0.0 copy-done.2
  110.0 2.0 fusion.1
  112.0 0.0 reduce-scatter.5.cloned.1.call-update
  112.0 0.0 reduce-scatter.9.cloned.1.call-start
  112.1 2.3 fusion.2
  114.4 0.0 reduce-scatter.9.cloned.1.call-update
  114.4 0.0 reduce-scatter.7.cloned.1.call-start
  114.4 20.2 %reduce-scatter.5.cloned.1.call-done = f32[16,2048]{1,0:T(8,128)} async-done(((f32[64,2048]{1,0:T(8,128)}), f32[16,2048]{1,0:T(8,128)}) %reduce-scatter.5.cloned.1.call-update) | async-done | bytes 131088 | tf_op jit(solution)/shard_map/reduce_scatter | solution.py:71
  134.7 0.0 reduce-scatter.7.cloned.1.call-update
  134.7 0.0 reduce-scatter.11.cloned.1.call-start
  134.7 26.3 %reduce-scatter.9.cloned.1.call-done = f32[16,3584]{1,0:T(8,128)} async-done(((f32[64,3584]{1,0:T(8,128)}), f32[16,3584]{1,0:T(8,128)}) %reduce-scatter.9.cloned.1.call-update) | async-done | bytes 229392 | tf_op jit(solution)/shard_map/reduce_scatter | solution.py:72
  161.0 0.0 reduce-scatter.11.cloned.1.call-update
  161.1 0.0 all-gather.6.cloned.1.call-start
  161.1 11.3 %reduce-scatter.7.cloned.1.call-done = f32[8,2048]{1,0:T(8,128)} async-done(((f32[16,2048]{1,0:T(8,128)}), f32[8,2048]{1,0:T(8,128)}) %reduce-scatter.7.cloned.1.call-update) | async-done | bytes 65552 | tf_op jit(solution)/shard_map/reduce_scatter | solution.py:75
  172.4 0.0 copy-done.4
  172.4 0.0 copy-done.7
  172.4 0.0 copy-done.8
  172.4 1.5 fusion.7
  173.9 32.9 %all_gather.25 = bf16[64,2048]{1,0:T(8,128)(2,1)} all-gather(bf16[8,2048]{1,0:T(8,128)(2,1)S(1)} %get-tuple-element.14), channel_id=1, replica_groups=mesh['role'=4,'dp'=2,'tp'=4] {'role','dp'}, dimensions={0}, use_global_device_ids=true | all-gather | bytes 294912 | tf_op jit(solution)/shard_map/all_gather | solution.py:88
  206.8 0.0 all-gather.6.cloned.1.call-update
  206.8 0.0 all-gather.4.cloned.1.call-start
  206.9 0.0 reduce-scatter.11.cloned.1.call-done
  206.9 0.0 copy-done.3
  206.9 0.0 copy-done.5
  206.9 0.0 copy-done.6
  206.9 1.7 fusion.6
  208.6 33.1 %all_gather.23 = bf16[64,3584]{1,0:T(8,128)(2,1)} all-gather(bf16[8,3584]{1,0:T(8,128)(2,1)S(1)} %get-tuple-element.10), channel_id=1, replica_groups=mesh['role'=4,'dp'=2,'tp'=4] {'role','dp'}, dimensions={0}, use_global_device_ids=true | all-gather | bytes 516096 | tf_op jit(solution)/shard_map/all_gather | solution.py:89
  241.7 0.0 all-gather.4.cloned.1.call-update
  241.7 0.0 all-gather.8.cloned.1.call-start
  241.7 0.7 all-gather.8.cloned.1.call-update
  242.5 0.0 all-gather.6.cloned.1.call-done
  242.5 20.4 %all-gather.4.cloned.1.call-done = bf16[64,14336]{1,0:T(8,128)(2,1)} async-done(((bf16[64,3584]{1,0:T(8,128)(2,1)}), bf16[64,14336]{1,0:T(8,128)(2,1)}) %all-gather.4.cloned.1.call-update) | async-done | bytes 1835024 | tf_op jit(solution)/shard_map/all_gather | solution.py:93
  262.9 23.8 %add_convert_fusion = bf16[1792,8192]{1,0:T(8,128)(2,1)} fusion(bf16[1792,8192]{1,0:T(8,128)(2,1)} %param.20, bf16[64,8192]{1,0:T(8,128)(2,1)} %all-gather.6.cloned.1.call-done, bf16[64,14336]{1,0:T(8,128)(2,1)} %all-gather.4.cloned.1.call-done, s32[]{:T(128)S(6)} %select_n.3), kind=kOutput, calls=%fused_computation | convolution fusion | flops 1937768448 | bytes 59998212 | tf_op jit(solution)/shard_map/dot_general | solution.py:35
  286.7 14.7 %all-gather.8.cloned.1.call-done = bf16[256,8192]{1,0:T(8,128)(2,1)} async-done(((bf16[32,8192]{1,0:T(8,128)(2,1)}), bf16[256,8192]{1,0:T(8,128)(2,1)}) %all-gather.8.cloned.1.call-update) | async-done | bytes 4194320 | tf_op jit(solution)/shard_map/all_gather | solution.py:102
  301.4 0.0 copy-start.1
  301.4 15.4 %convolution_convert_fusion = bf16[1792,256]{1,0:T(8,128)(2,1)} fusion(bf16[1792,8192]{1,0:T(8,128)(2,1)} %add_convert_fusion, bf16[256,8192]{1,0:T(8,128)(2,1)} %all-gather.8.cloned.1.call-done), kind=kOutput, calls=%fused_computation.1 | convolution fusion | flops 7516651520 | bytes 34471936 | tf_op jit(solution)/shard_map/dot_general | solution.py:41
  316.8 0.0 copy-done.1
Async XLA Ops:
  7.2 65.6 %copy-start = (bf16[256,3584]{1,0:T(8,128)(2,1)S(1)}, bf16[256,3584]{1,0:T(8,128)(2,1)}, u32[]{:S(2)}) copy-start(bf16[256,3584]{1,0:T(8,128)(2,1)} %param.12) | copy-start | bytes 5505028
  7.2 102.8 %copy-start.2 = (bf16[256,2048]{1,0:T(8,128)(2,1)S(1)}, bf16[256,2048]{1,0:T(8,128)(2,1)}, u32[]{:S(2)}) copy-start(bf16[256,2048]{1,0:T(8,128)(2,1)} %param.11) | copy-start | bytes 3145732
  7.2 102.8 %all-reduce.3.cloned.1.call-start = ((), (), s32[]{:S(2)}) async-start(), calls=%async_computation.11 | async-start | bytes 524288 | tf_op jit(solution)/shard_map/psum | solution.py:65
  74.0 98.4 %copy-start.4 = (f32[8,2048]{1,0:T(8,128)S(1)}, f32[8,2048]{1,0:T(8,128)}, u32[]{:S(2)}) copy-start(f32[8,2048]{1,0:T(8,128)} %param.14) | copy-start | bytes 196612
  74.0 98.4 %copy-start.7 = (f32[8,2048]{1,0:T(8,128)S(1)}, f32[8,2048]{1,0:T(8,128)}, u32[]{:S(2)}) copy-start(f32[8,2048]{1,0:T(8,128)} %param.15) | copy-start | bytes 196612
  74.0 98.4 %copy-start.8 = (f32[8,2048]{1,0:T(8,128)S(1)}, f32[8,2048]{1,0:T(8,128)}, u32[]{:S(2)}) copy-start(f32[8,2048]{1,0:T(8,128)} %param.16) | copy-start | bytes 196612
  76.4 130.6 %copy-start.3 = (f32[8,3584]{1,0:T(8,128)S(1)}, f32[8,3584]{1,0:T(8,128)}, u32[]{:S(2)}) copy-start(f32[8,3584]{1,0:T(8,128)} %param.17) | copy-start | bytes 344068
  76.4 130.6 %copy-start.5 = (f32[8,3584]{1,0:T(8,128)S(1)}, f32[8,3584]{1,0:T(8,128)}, u32[]{:S(2)}) copy-start(f32[8,3584]{1,0:T(8,128)} %param.18) | copy-start | bytes 344068
  76.4 130.6 %copy-start.6 = (f32[8,3584]{1,0:T(8,128)S(1)}, f32[8,3584]{1,0:T(8,128)}, u32[]{:S(2)}) copy-start(f32[8,3584]{1,0:T(8,128)} %param.19) | copy-start | bytes 344068
  76.4 58.3 %reduce-scatter.5.cloned.1.call-start = ((), (), s32[]{:S(2)}) async-start(), calls=%async_computation.4 | async-start | bytes 655360 | tf_op jit(solution)/shard_map/reduce_scatter | solution.py:71
  112.0 49.0 %reduce-scatter.9.cloned.1.call-start = ((), (), s32[]{:S(2)}) async-start(), calls=%async_computation.6 | async-start | bytes 1146880 | tf_op jit(solution)/shard_map/reduce_scatter | solution.py:72
  114.4 58.0 %reduce-scatter.7.cloned.1.call-start = ((), (), s32[]{:S(2)}) async-start(), calls=%async_computation.5 | async-start | bytes 196608 | tf_op jit(solution)/shard_map/reduce_scatter | solution.py:75
  134.7 72.2 %reduce-scatter.11.cloned.1.call-start = ((), (), s32[]{:S(2)}) async-start(), calls=%async_computation.7 | async-start | bytes 344064 | tf_op jit(solution)/shard_map/reduce_scatter | solution.py:76
  161.1 81.4 %all-gather.6.cloned.1.call-start = ((), (), s32[]{:S(2)}) async-start(), calls=%async_computation.9 | async-start | bytes 1310720 | tf_op jit(solution)/shard_map/all_gather | solution.py:92
  206.8 56.1 %all-gather.4.cloned.1.call-start = ((), (), s32[]{:S(2)}) async-start(), calls=%async_computation.8 | async-start | bytes 2293760 | tf_op jit(solution)/shard_map/all_gather | solution.py:93
  241.7 59.7 %all-gather.8.cloned.1.call-start = ((), (), s32[]{:S(2)}) async-start(), calls=%async_computation.10 | async-start | bytes 4718592 | tf_op jit(solution)/shard_map/all_gather | solution.py:102
  301.4 15.4 %copy-start.1 = (bf16[256,3584]{1,0:T(8,128)(2,1)S(1)}, bf16[256,3584]{1,0:T(8,128)(2,1)}, u32[]{:S(2)}) copy-start(bf16[256,3584]{1,0:T(8,128)(2,1)} %param.12) | copy-start | bytes 5505028
Sparse Core Ops, SparseCore 0:
  76.5 33.4 all-reduce.2
  112.8 21.8 reduce-scatter.4
  137.6 23.4 reduce-scatter.8
  163.1 9.2 reduce-scatter.6
  174.5 11.9 reduce-scatter.10
  207.0 16.5 all-gather.5
  241.8 21.0 all-gather.3
  264.8 36.5 all-gather.7
where the time goes:
time: 324 us
  blocking collectives  130 us (40%)
  waiting for transfers between devices  127 us (39%)
  matrix products  47.2 us (15%)
  between operations  14.9 us (5%)
  other arithmetic  5.1 us (2%)
    all_gather x1, blocking collectives, body(): lax.all_gather(output_send, ('role', 'dp'), axis=0, tiled=True)  33.1 us
    all_gather x1, blocking collectives, body(): lax.all_gather(input_send, ('role', 'dp'), axis=0, tiled=True)  32.9 us
    all_gather x1, blocking collectives, body(): lax.all_gather(output_factor.astype(jnp.bfloat16), ('role', 'dp'), axis=0...  32.9 us
    psum x1, waiting for transfers between devices, body(): low_input, low_grad = lax.psum((low_input, low_grad), 'tp')  32.8 us
    all_gather x1, blocking collectives, body(): lax.all_gather(input_factor.astype(jnp.bfloat16), ('role', 'dp'), axis=0,...  30.7 us
    dot_general x3, matrix products, contract_rows(): lax.dot_general(left, right, (((0,), (0,)), ((), ())), preferred_element_...  28.1 us
    reduce_scatter x1, waiting for transfers between devices, body(): lax.psum_scatter(output_part, 'role', scatter_dimension=0, tiled=True)  26.3 us
    all_gather x1, waiting for transfers between devices, body(): lax.all_gather(output_cols, 'tp', axis=1, tiled=True)  20.4 us
  transfers between devices with their start and end apart: 8, of which 6 were waited for; matrix products, arithmetic and copies ran while one was open for 9% of the time, Pallas kernels for 0%

commit v1 on v0

v1 whole, which is shorter than its diff:
```python
import functools

import jax
import jax.numpy as jnp
from jax import lax
from jax.experimental import pallas as pl
from jax.experimental.pallas import tpu as pltpu
from jax.sharding import PartitionSpec as P

ROLLOUT_TOKENS = 256

adapter_scale = 2.0
learn_rate = 0.004
beta_one = 0.9
beta_two = 0.95
epsilon = 1e-08
first_fix = 1.0 - 0.9**20
second_fix = 1.0 - 0.95**20

F32 = jnp.float32
BF16 = jnp.bfloat16
VMEM = pltpu.VMEM
MIB = 1024 * 1024


def adam_update(factor, moment, square, gradient):
    moment_new = beta_one * moment + (1.0 - beta_one) * gradient
    square_new = beta_two * square + (1.0 - beta_two) * gradient * gradient
    factor_new = factor - learn_rate * (moment_new / first_fix) / (
        jnp.sqrt(square_new / second_fix) + epsilon
    )
    return (factor_new, moment_new, square_new)


def contract_rows(left, right):
    return lax.dot_general(
        left, right, (((0,), (0,)), ((), ())), preferred_element_type=F32
    )


def contract_cols(left, right):
    return lax.dot_general(
        left, right, (((1,), (1,)), ((), ())), preferred_element_type=F32
    )


def masked(values, block_keep):
    blocks = block_keep.shape[0]
    reshaped_rows = values.reshape(blocks, values.shape[0] // blocks, values.shape[1])
    weighted = reshaped_rows * block_keep.astype(F32)[:, None, None]
    return weighted.reshape(values.shape).astype(BF16)


def plain_body(
    activations,
    cotangent,
    block_keep,
    input_factor,
    input_mean,
    input_square,
    output_factor,
    output_mean,
    output_square,
    frozen_base_rows,
    prompts,
):
    input_rows, output_rows = (
        lax.all_gather(input_factor.astype(BF16), ("role", "dp"), axis=0, tiled=True),
        lax.all_gather(output_factor.astype(BF16), ("role", "dp"), axis=0, tiled=True),
    )
    low_input = jnp.dot(activations, input_rows.T, preferred_element_type=F32)
    low_grad = jnp.dot(cotangent, output_rows.T, preferred_element_type=F32)
    low_input, low_grad = lax.psum((low_input, low_grad), "tp")
    input_kept = masked(low_input, block_keep)
    grad_kept = masked(low_grad, block_keep)
    input_part = contract_rows(grad_kept, activations)
    output_part = contract_rows(input_kept, cotangent)
    group_input, group_output = (
        lax.psum_scatter(input_part, "role", scatter_dimension=0, tiled=True),
        lax.psum_scatter(output_part, "role", scatter_dimension=0, tiled=True),
    )
    input_sum, output_sum = (
        lax.psum_scatter(group_input, "dp", scatter_dimension=0, tiled=True),
        lax.psum_scatter(group_output, "dp", scatter_dimension=0, tiled=True),
    )
    factor_scale = adapter_scale / ROLLOUT_TOKENS
    input_new, input_moment, input_second = adam_update(
        input_factor, input_mean, input_square, input_sum * factor_scale
    )
    output_new, output_moment, output_second = adam_update(
        output_factor, output_mean, output_square, output_sum * factor_scale
    )
    input_cols, output_cols = (
        lax.all_gather(input_new.astype(BF16), ("role", "dp"), axis=0, tiled=True),
        lax.all_gather(output_new.astype(BF16), ("role", "dp"), axis=0, tiled=True),
    )
    input_whole, output_whole = (
        lax.all_gather(input_cols, "tp", axis=1, tiled=True),
        lax.all_gather(output_cols, "tp", axis=1, tiled=True),
    )
    rows_here = frozen_base_rows.shape[0]
    row_block = lax.axis_index("dp") * lax.axis_size("tp") + lax.axis_index("tp")
    output_slice = lax.dynamic_slice_in_dim(
        output_whole, row_block * rows_here, rows_here, 1
    )
    adapter_delta_rows = contract_rows(output_slice, input_whole)
    merged_weight_rows = (
        frozen_base_rows.astype(F32) + adapter_scale * adapter_delta_rows
    ).astype(BF16)
    group_prompts = lax.all_gather(prompts, ("dp", "tp"), axis=0, tiled=True)
    projected = contract_cols(merged_weight_rows, group_prompts)
    return (
        input_new,
        output_new,
        input_moment,
        output_moment,
        input_second,
        output_second,
        merged_weight_rows,
        projected.astype(BF16),
    )


def swap(value, axis, size, step):
    return lax.ppermute(value, axis, [(i, i ^ step) for i in range(size)])


def params(mib):
    return pltpu.CompilerParams(vmem_limit_bytes=mib * MIB)


def cost(flops, nbytes):
    return pl.CostEstimate(flops=flops, bytes_accessed=nbytes, transcendentals=0)


def whole():
    return pl.BlockSpec(memory_space=VMEM)


def low_kernel(count, width, *refs):
    pieces, (act, cot, out) = refs[:count], refs[count:]
    rank = out.shape[0] // 2
    left = jnp.concatenate([p[:, :width].astype(F32) for p in pieces], 0).astype(BF16)
    right = jnp.concatenate([p[:, width:].astype(F32) for p in pieces], 0).astype(BF16)
    out[:rank] = contract_cols(left, act[...])
    out[rank:] = contract_cols(right, cot[...])


def grad_kernel(count, width, keep, *refs):
    parts = refs[: len(refs) - 2 - count]
    act, cot = refs[len(parts) : len(parts) + 2]
    outs = refs[len(parts) + 2 :]
    low = parts[0][...]
    for part in parts[1:]:
        low = low + part[...]
    kept = (low * keep[0].astype(F32)).astype(BF16)
    rank = kept.shape[0] // 2
    rows = rank // count
    input_part = jnp.dot(kept[rank:], act[...], preferred_element_type=F32)
    output_part = jnp.dot(kept[:rank], cot[...], preferred_element_type=F32)
    for k, out in enumerate(outs):
        span = slice(k * rows, (k + 1) * rows)
        out[:, :width] = input_part[span].astype(out.dtype)
        out[:, width:] = output_part[span].astype(out.dtype)


def adam_kernel(count, width, place, *refs):
    parts = refs[:count]
    fa, ma, va, fb, mb, vb = refs[count : count + 6]
    nfa, nfb, nma, nmb, nva, nvb, send_a = refs[count + 6 : count + 13]
    send_b, hold = refs[count + 13 : -1], refs[-1]
    total = parts[0][...]
    for part in parts[1:]:
        total = total + part[...].astype(F32)
    total = total * (adapter_scale / ROLLOUT_TOKENS)
    nfa[...], nma[...], nva[...] = adam_update(
        fa[...], ma[...], va[...], total[:, :width]
    )
    nfb[...], nmb[...], nvb[...] = adam_update(
        fb[...], mb[...], vb[...], total[:, width:]
    )
    send_a[...] = nfa[...].astype(BF16)
    hold[...] = nfb[...]
    wide = send_b[0].shape[1]
    for k, out in enumerate(send_b):
        start = pl.multiple_of((place[0] ^ k) * wide, 128)
        out[...] = hold[:, pl.ds(start, wide)].astype(BF16)


def join_kernel(width, *refs):
    pieces, (out_a, out_b) = refs[:-2], refs[-2:]
    whole_rows = jnp.concatenate([p[...].astype(F32) for p in pieces], 0).astype(BF16)
    out_a[...] = whole_rows[:, :width]
    out_b[...] = whole_rows[:, width:]


def early_kernel(count, place, *refs):
    pieces, (base, early, wide, sem) = refs[:count], refs[count:]

    @pl.when(pl.program_id(0) == 0)
    def _():
        rows = pieces[0].shape[0]
        copies = []
        for k, piece in enumerate(pieces):
            start = pl.multiple_of(place[k] * rows, rows)
            copies.append(
                pltpu.make_async_copy(piece, wide.at[pl.ds(start, rows)], sem.at[k])
            )
        for copy in copies:
            copy.start()
        for copy in copies:
            copy.wait()

    early[...] = contract_cols(base[...], wide[...])


def merge_kernel(first, last, slot, *refs):
    refs = list(refs)
    a, b, base, wide = refs[:4]
    rest = refs[4:]
    if not first:
        rest = rest[1:]
        seen, rest = rest[0], rest[1:]
    if last:
        early, rest = rest[0], rest[1:]
    merged, low = rest[0], rest[1]
    here = contract_cols(a[...], wide[...])

    @pl.when(pl.program_id(0) == 0)
    def _():
        low[...] = here if first else here + seen[...]

    delta = contract_rows(b[...], a[...])
    merged[...] = (base[...].astype(F32) + adapter_scale * delta).astype(BF16)
    if last:
        full = low[...]
        high = full.astype(BF16)
        rest_low = (full - high.astype(F32)).astype(BF16)
        twice = jnp.concatenate([b[...], b[...]], 0)
        both = jnp.concatenate([high, rest_low], 0)
        rest[2][...] = (early[...] + adapter_scale * contract_rows(twice, both)).astype(
            BF16
        )


def exchange_body(
    sizes,
    activations,
    cotangent,
    block_keep,
    input_factor,
    input_mean,
    input_square,
    output_factor,
    output_mean,
    output_square,
    frozen_base_rows,
    prompts,
):
    roles, dps, tps = sizes
    both = ("role", "dp")
    owners = roles * dps
    tokens, width = activations.shape
    hidden = cotangent.shape[1]
    rows = input_factor.shape[0]
    rank = rows * owners
    base_rows, model = frozen_base_rows.shape
    asked = prompts.shape[0]
    d, t = lax.axis_index("dp"), lax.axis_index("tp")
    struct = jax.ShapeDtypeStruct

    mine = jnp.concatenate([input_factor.astype(BF16), output_factor.astype(BF16)], 1)
    pieces = [mine] + [swap(mine, both, owners, k) for k in range(1, owners)]
    low = pl.pallas_call(
        functools.partial(low_kernel, owners, width),
        out_shape=struct((2 * rank, tokens), F32),
        in_specs=[whole()] * (owners + 2),
        out_specs=whole(),
        compiler_params=params(24),
        cost_estimate=cost(2 * rank * tokens * (width + hidden), 4 * MIB),
        name="low",
    )(*pieces, activations, cotangent)
    lows = [low] + [swap(low, "tp", tps, k) for k in range(1, tps)]

    grads = pl.pallas_call(
        functools.partial(grad_kernel, owners, width),
        out_shape=[struct((rows, width + hidden), F32)]
        + [struct((rows, width + hidden), BF16)] * (owners - 1),
        in_specs=[pl.BlockSpec(memory_space=pltpu.SMEM)] + [whole()] * (tps + 2),
        out_specs=[whole()] * owners,
        compiler_params=params(24),
        cost_estimate=cost(2 * rank * tokens * (width + hidden), 4 * MIB),
        name="grad",
    )(block_keep, *lows, activations, cotangent)
    parts = [grads[0]] + [
        swap(grads[k], both, owners, k) for k in range(1, owners)
    ]

    share = hidden // dps
    small_a, small_b = struct((rows, width), F32), struct((rows, hidden), F32)
    adam = pl.pallas_call(
        functools.partial(adam_kernel, owners, width),
        out_shape=[small_a, small_b] * 3
        + [struct((rows, width), BF16)]
        + [struct((rows, share), BF16)] * dps,
        in_specs=[pl.BlockSpec(memory_space=pltpu.SMEM)] + [whole()] * (owners + 6),
        out_specs=[whole()] * (7 + dps),
        scratch_shapes=[VMEM((rows, hidden), F32)],
        compiler_params=params(16),
        cost_estimate=cost(40 * rows * (width + hidden), 4 * MIB),
        name="adam",
    )(
        d[None],
        *parts,
        input_factor,
        input_mean,
        input_square,
        output_factor,
        output_mean,
        output_square,
    )
    outs, send_a, send_b = adam[:6], adam[6], adam[7:]

    near_a = [send_a] + [swap(send_a, "dp", dps, k) for k in range(1, dps)]
    near_b = [
        lax.ppermute(
            send_b[k],
            ("dp", "tp"),
            [
                (i, (i % tps) * dps + ((i // tps) ^ k))
                for i in range(dps * tps)
            ],
        )
        for k in range(dps)
    ]
    turn = d ^ ((d * tps + t) % dps)
    stacked = jnp.stack(near_b, 0)
    ordered = [
        lax.dynamic_index_in_dim(stacked, turn ^ k, 0, keepdims=False)
        for k in range(dps)
    ]
    plane = jnp.concatenate(
        [jnp.concatenate([near_a[k], ordered[k]], 1) for k in range(dps)], 0
    )
    planes = [plane] + [swap(plane, "role", roles, k) for k in range(1, roles)]
    a_own, b_here = pl.pallas_call(
        functools.partial(join_kernel, width),
        out_shape=[struct((rank, width), BF16), struct((rank, share), BF16)],
        in_specs=[whole()] * roles,
        out_specs=[whole()] * 2,
        compiler_params=params(8),
        cost_estimate=cost(rank * width, MIB),
        name="join",
    )(*planes)
    slots = {0: a_own}
    step = 1
    while step < tps:
        step *= 2
    held = [0]
    step //= 2
    order = [0]
    reach = []
    k = 1
    while k < tps:
        reach.append(k)
        k *= 2
    for k in range(1, tps):
        top = max(bit for bit in reach if k & bit)
        low_part = k ^ top
        if low_part:
            slots[k] = swap(slots[top], "tp", tps, low_part)
        else:
            slots[k] = swap(a_own, "tp", tps, top)

    asks = {(0, 0): prompts}
    for kd in range(1, dps):
        asks[kd, 0] = swap(prompts, "dp", dps, kd)
    for kd in range(dps):
        for k in reversed(reach):
            for kt in [kt for (od, kt) in list(asks) if od == kd]:
                asks[kd, kt ^ k] = swap(asks[kd, kt], "tp", tps, k)
    keys = sorted(asks)
    spots = jnp.stack([(d ^ kd) * tps + (t ^ kt) for kd, kt in keys])
    gathered = asked * len(keys)
    tile = 256 if base_rows % 256 == 0 else base_rows
    early, wide = pl.pallas_call(
        functools.partial(early_kernel, len(keys)),
        out_shape=[struct((base_rows, gathered), F32), struct((gathered, model), BF16)],
        grid=(base_rows // tile,),
        in_specs=[pl.BlockSpec(memory_space=pltpu.SMEM)]
        + [pl.BlockSpec(memory_space=pl.ANY)] * len(keys)
        + [pl.BlockSpec((tile, model), lambda i: (i, 0))],
        out_specs=[
            pl.BlockSpec((tile, gathered), lambda i: (i, 0)),
            pl.BlockSpec((gathered, model), lambda i: (0, 0)),
        ],
        scratch_shapes=[pltpu.SemaphoreType.DMA((len(keys),))],
        compiler_params=params(40),
        cost_estimate=cost(
            2 * base_rows * gathered * model, 2 * (base_rows + 2 * gathered) * model
        ),
        name="early",
    )(spots, *[asks[key] for key in keys], frozen_base_rows)

    merged = low_sum = None
    for k in range(tps):
        first, last = k == 0, k == tps - 1
        args = [slots[k], b_here, frozen_base_rows, wide]
        specs = [
            pl.BlockSpec((rank, width), lambda i, s: (0, 0)),
            pl.BlockSpec((rank, tile), lambda i, s: (0, i)),
            pl.BlockSpec((tile, width), lambda i, s: (i, s[0])),
            pl.BlockSpec((gathered, width), lambda i, s: (0, s[0])),
        ]
        alias = {}
        out_shape = [
            struct((base_rows, model), BF16),
            struct((rank, gathered), F32),
        ]
        out_specs = [
            pl.BlockSpec((tile, width), lambda i, s: (i, s[0])),
            pl.BlockSpec((rank, gathered), lambda i, s: (0, 0)),
        ]
        if not first:
            args += [merged, low_sum]
            specs += [
                pl.BlockSpec(memory_space=pl.ANY),
                pl.BlockSpec((rank, gathered), lambda i, s: (0, 0)),
            ]
            alias = {5: 0}
        if last:
            args.append(early)
            specs.append(pl.BlockSpec((tile, gathered), lambda i, s: (i, 0)))
            out_shape.append(struct((base_rows, gathered), BF16))
            out_specs.append(pl.BlockSpec((tile, gathered), lambda i, s: (i, 0)))
        results = pl.pallas_call(
            functools.partial(merge_kernel, first, last),
            out_shape=out_shape,
            grid_spec=pltpu.PrefetchScalarGridSpec(
                num_scalar_prefetch=1,
                grid=(base_rows // tile,),
                in_specs=specs,
                out_specs=out_specs,
            ),
            input_output_aliases=alias,
            compiler_params=params(24),
            cost_estimate=cost(
                2 * base_rows * rank * width, 4 * base_rows * width
            ),
            name=f"merge{k}",
        )((t ^ k)[None], *args)
        merged, low_sum = results[0], results[1]
    projected = results[2]
    return (*outs, merged, projected)


def power_of_two(n):
    return n & (n - 1) == 0


def solution(mesh):
    roles, dps, tps = (mesh.shape[name] for name in ("role", "dp", "tp"))
    small = roles * dps <= 8 and 1 < tps <= 8 and tps % dps == 0
    if small and all(power_of_two(n) for n in (roles, dps, tps)):
        body = functools.partial(exchange_body, (roles, dps, tps))
    else:
        body = plain_body
    owned = P(("role", "dp"), "tp")
    return jax.shard_map(
        body,
        mesh=mesh,
        in_specs=(
            owned,
            owned,
            P(("role", "dp")),
            *[owned] * 6,
            P(("dp", "tp"), None),
            P(("role", "dp", "tp"), None),
        ),
        out_specs=(
            *[owned] * 6,
            P(("dp", "tp"), None),
            P(("dp", "tp"), "role"),
        ),
        check_vma=False,
    )
```

time: 324 us -> 182 us (0.56)
  blocking collectives: 130 us -> 0 us
  waiting for transfers between devices: 127 us -> 50.4 us
  Pallas kernels: 0 us -> 63.7 us
  starting transfers between devices: 0.32 us -> 51.7 us
  matrix products: 47.2 us -> 0 us
  between operations: 14.9 us -> 1.4 us
  local copies, waits for them, and re-layouts: 0.04 us -> 11.8 us
  other arithmetic: 5.1 us -> 1.8 us
    all_gather x4 -> x0, blocking collectives: 130 us -> none  [the longest x1 33.1 us: body(): lax.all_gather(output_send, ('role', 'dp'), axis=0, tiled=True)]
    pallas_call x0 -> x9, Pallas kernels: none -> 63.7 us  [the longest x4 44.7 us: exchange_body(): pl.pallas_call(functools.partial(merge_kernel, first, last), out_shape=ou...]
    reduce_scatter x4 -> x0, waiting for transfers between devices: 57.8 us -> none  [the longest x1 26.3 us: body(): lax.psum_scatter(output_part, 'role', scatter_dimension=0, tiled=True)]
    ppermute x0 -> x33, starting transfers between devices: none -> 51.7 us  [the longest x31 48.9 us: swap(): return lax.ppermute(value, axis, [(i, i ^ step) for i in range(size)])]
    ppermute x0 -> x33, waiting for transfers between devices: none -> 50.4 us  [the longest x31 50.3 us: swap(): return lax.ppermute(value, axis, [(i, i ^ step) for i in range(size)])]
    dot_general x6 -> x0, matrix products: 47.2 us -> none  [the longest x3 28.1 us: contract_rows(): lax.dot_general(left, right, (((0,), (0,)), ((), ())), preferred_element_...]
    all_gather x3 -> x0, waiting for transfers between devices: 35.1 us -> none  [the longest x1 20.4 us: body(): lax.all_gather(output_cols, 'tp', axis=1, tiled=True)]
    psum x1 -> x0, waiting for transfers between devices: 32.8 us -> none  [body(): low_input, low_grad = lax.psum((low_input, low_grad), 'tp')]
  transfers between devices with their start and end apart: 8 -> 33, of which waited for: 6 -> 12; matrix products, arithmetic and copies ran while one was open for 9% -> 0% of each run, Pallas kernels for 0% -> 29%
where the time goes in v1:
time: 182 us; the launch traced here: 181 us
  Pallas kernels  63.7 us (35%)
  starting transfers between devices  51.7 us (28%)
  waiting for transfers between devices  50.4 us (28%)
  local copies, waits for them, and re-layouts  11.8 us (6%)
    ppermute x31, waiting for transfers between devices, swap(): return lax.ppermute(value, axis, [(i, i ^ step) for i in range(size)])  50.3 us
    ppermute x31, starting transfers between devices, swap(): return lax.ppermute(value, axis, [(i, i ^ step) for i in range(size)])  48.9 us
    pallas_call x4, Pallas kernels, exchange_body(): pl.pallas_call(functools.partial(merge_kernel, first, last), out_shape=ou...  44.7 us
    pallas_call x1, Pallas kernels, exchange_body(): pl.pallas_call(functools.partial(early_kernel, len(keys)), out_shape=[str...  15.7 us
    unnamed x22, local copies, waits for them, and re-layouts  11.7 us
  transfers between devices with their start and end apart: 33, of which 12 were waited for; matrix products, arithmetic and copies ran while one was open for 0% of the time, Pallas kernels for 29%

profile of v1, /device:TPU:0, one launch (start us, length us, event | category | flops | bytes accessed | tf_op | source)
XLA Modules:
  0.0 180.7 jit_solution(15779121729948957931)
XLA Ops:
  0.6 0.8 convert_element_type.6
  1.5 0.9 convert_element_type.7
  2.4 6.1 %collective-permute-start.6 = (bf16[8,5632]{1,0:T(8,128)(2,1)S(1)}, bf16[8,5632]{1,0:T(8,128)(2,1)S(1)}, u32[]{:S(2)}, u32[]{:S(2)}) collective-permute-start(bf16[8,5632]{1,0:T(8,128)(2,1)S(1)} %pad_maximum_fusion.refs_0_), channel_id=1, source_target_pairs={{0,28},{4,24},{8,20},{12,16},{16,12},{20,8},{24,4},{28,0},{1,29},{... | collective-permute-start | bytes 270344 | tf_op jit(solution)/shard_map/ppermute | solution.py:125
  8.5 0.2 collective-permute-start.5
  8.7 0.8 collective-permute-start.4
  9.5 2.0 %collective-permute-start.3 = (bf16[8,5632]{1,0:T(8,128)(2,1)S(1)}, bf16[8,5632]{1,0:T(8,128)(2,1)S(1)}, u32[]{:S(2)}, u32[]{:S(2)}) collective-permute-start(bf16[8,5632]{1,0:T(8,128)(2,1)S(1)} %pad_maximum_fusion.refs_0_), channel_id=1, source_target_pairs={{0,16},{4,20},{8,24},{12,28},{16,0},{20,4},{24,8},{28,12},{1,17},{... | collective-permute-start | bytes 270344 | tf_op jit(solution)/shard_map/ppermute | solution.py:125
  11.5 2.3 %collective-permute-start.2 = (bf16[8,5632]{1,0:T(8,128)(2,1)S(1)}, bf16[8,5632]{1,0:T(8,128)(2,1)S(1)}, u32[]{:S(2)}, u32[]{:S(2)}) collective-permute-start(bf16[8,5632]{1,0:T(8,128)(2,1)S(1)} %pad_maximum_fusion.refs_0_), channel_id=1, source_target_pairs={{0,12},{4,8},{8,4},{12,0},{16,28},{20,24},{24,20},{28,16},{1,13},{... | collective-permute-start | bytes 270344 | tf_op jit(solution)/shard_map/ppermute | solution.py:125
  13.8 5.0 %collective-permute-start.1 = (bf16[8,5632]{1,0:T(8,128)(2,1)S(1)}, bf16[8,5632]{1,0:T(8,128)(2,1)S(1)}, u32[]{:S(2)}, u32[]{:S(2)}) collective-permute-start(bf16[8,5632]{1,0:T(8,128)(2,1)S(1)} %pad_maximum_fusion.refs_0_), channel_id=1, source_target_pairs={{0,8},{4,12},{8,0},{12,4},{16,24},{20,28},{24,16},{28,20},{1,9},{5... | collective-permute-start | bytes 270344 | tf_op jit(solution)/shard_map/ppermute | solution.py:125
  18.8 1.4 collective-permute-start
  20.2 2.7 %collective-permute-done.4.refs_5_ = bf16[8,5632]{1,0:T(8,128)(2,1)S(1)} collective-permute-done((bf16[8,5632]{1,0:T(8,128)(2,1)S(1)}, bf16[8,5632]{1,0:T(8,128)(2,1)S(1)}, u32[]{:S(2)}, u32[]{:S(2)}) %collective-permute-start.4) | collective-permute-done | bytes 90144 | tf_op jit(solution)/shard_map/ppermute | solution.py:125
  22.8 1.0 collective-permute-done.3.refs_4_
  23.9 0.6 collective-permute-done.1.refs_2_
  24.5 1.5 copy-done
  26.0 1.2 copy-done.2
  27.2 1.0 low.1.refs_0_
  28.2 0.1 collective-permute-start.9
  28.3 1.6 collective-permute-start.8
  29.9 0.3 collective-permute-start.7
  30.1 0.8 collective-permute-start.28
  31.6 2.4 %collective-permute-done.9.refs_3_ = f32[128,256]{1,0:T(8,128)S(1)} collective-permute-done((f32[128,256]{1,0:T(8,128)S(1)}, f32[128,256]{1,0:T(8,128)S(1)}, u32[]{:S(2)}, u32[]{:S(2)}) %collective-permute-start.9) | collective-permute-done | bytes 131104 | tf_op jit(solution)/shard_map/ppermute | solution.py:125
  34.0 2.9 %collective-permute-done.8.refs_2_ = f32[128,256]{1,0:T(8,128)S(1)} collective-permute-done((f32[128,256]{1,0:T(8,128)S(1)}, f32[128,256]{1,0:T(8,128)S(1)}, u32[]{:S(2)}, u32[]{:S(2)}) %collective-permute-start.8) | collective-permute-done | bytes 131104 | tf_op jit(solution)/shard_map/ppermute | solution.py:125
  36.9 1.5 copy-done.1
  38.4 1.2 copy-done.3
  39.6 0.6 grad.1
  40.2 0.8 collective-permute-start.10
  41.1 1.2 collective-permute-start.11
  42.3 1.5 collective-permute-start.12
  43.8 2.6 %collective-permute-start.13 = (bf16[8,5632]{1,0:T(8,128)(2,1)S(1)}, bf16[8,5632]{1,0:T(8,128)(2,1)S(1)}, u32[]{:S(2)}, u32[]{:S(2)}) collective-permute-start(bf16[8,5632]{1,0:T(8,128)(2,1)S(1)} %get-tuple-element.41), channel_id=1, source_target_pairs={{0,16},{4,20},{8,24},{12,28},{16,0},{20,4},{24,8},{28,12},{1,17},{... | collective-permute-start | bytes 270344 | tf_op jit(solution)/shard_map/ppermute | solution.py:125
  46.4 0.7 collective-permute-done.10.refs_1_
  47.1 2.7 %collective-permute-start.14 = (bf16[8,5632]{1,0:T(8,128)(2,1)S(1)}, bf16[8,5632]{1,0:T(8,128)(2,1)S(1)}, u32[]{:S(2)}, u32[]{:S(2)}) collective-permute-start(bf16[8,5632]{1,0:T(8,128)(2,1)S(1)} %get-tuple-element.42), channel_id=1, source_target_pairs={{0,20},{4,16},{8,28},{12,24},{16,4},{20,0},{24,12},{28,8},{1,21},{... | collective-permute-start | bytes 270344 | tf_op jit(solution)/shard_map/ppermute | solution.py:125
  49.9 1.2 collective-permute-start.15
  51.1 3.6 %collective-permute-start.16 = (bf16[8,5632]{1,0:T(8,128)(2,1)S(1)}, bf16[8,5632]{1,0:T(8,128)(2,1)S(1)}, u32[]{:S(2)}, u32[]{:S(2)}) collective-permute-start(bf16[8,5632]{1,0:T(8,128)(2,1)S(1)} %get-tuple-element.44), channel_id=1, source_target_pairs={{0,28},{4,24},{8,20},{12,16},{16,12},{20,8},{24,4},{28,0},{1,29},{... | collective-permute-start | bytes 270344 | tf_op jit(solution)/shard_map/ppermute | solution.py:125
  54.7 5.1 %collective-permute-done.14.refs_5_ = bf16[8,5632]{1,0:T(8,128)(2,1)S(1)} collective-permute-done((bf16[8,5632]{1,0:T(8,128)(2,1)S(1)}, bf16[8,5632]{1,0:T(8,128)(2,1)S(1)}, u32[]{:S(2)}, u32[]{:S(2)}) %collective-permute-start.14) | collective-permute-done | bytes 90144 | tf_op jit(solution)/shard_map/ppermute | solution.py:125
  59.8 0.9 copy-done.5
  60.7 0.8 copy-done.6
  61.6 0.9 copy-done.7
  62.5 0.9 copy-done.8
  63.4 0.8 copy-done.9
  64.2 0.8 copy-done.10
  65.0 1.0 adam.1
  66.0 0.7 collective-permute-start.17
  66.7 2.2 %collective-permute-start.18 = (bf16[8,1792]{1,0:T(8,128)(2,1)S(1)}, bf16[8,1792]{1,0:T(8,128)(2,1)S(1)}, u32[]{:S(2)}, u32[]{:S(2)}) collective-permute-start(bf16[8,1792]{1,0:T(8,128)(2,1)S(1)} %get-tuple-element.53), channel_id=1, source_target_pairs={{0,1},{1,3},{2,5},{3,7},{4,0},{5,2},{6,4},{7,6},{8,9},{9,11},{10,1... | collective-permute-start | bytes 86024 | tf_op jit(solution)/shard_map/ppermute | solution.py:326
  68.8 1.4 collective-permute-start.26
  70.3 0.5 collective-permute-start.19
  70.9 3.7 %collective-permute-start.30 = (bf16[32,8192]{1,0:T(8,128)(2,1)S(1)}, bf16[32,8192]{1,0:T(8,128)(2,1)S(1)}, u32[]{:S(2)}, u32[]{:S(2)}) collective-permute-start(bf16[32,8192]{1,0:T(8,128)(2,1)S(1)} %collective-permute-done.28.refs_4_), channel_id=1, source_target_pairs={{0,2},{1,3},{2,0},{3,1},{4,6},{5,7},{6,4},{7,5},{8,10},{9,11},{10,... | collective-permute-start | bytes 1572872 | tf_op jit(solution)/shard_map/ppermute | solution.py:125
  74.6 2.7 %collective-permute-start.22 = (bf16[16,3840]{1,0:T(8,128)(2,1)S(1)}, bf16[16,3840]{1,0:T(8,128)(2,1)S(1)}, u32[]{:S(2)}, u32[]{:S(2)}) collective-permute-start(bf16[16,3840]{1,0:T(8,128)(2,1)S(1)} %maximum_maximum_fusion.refs_0_), channel_id=1, source_target_pairs={{0,24},{8,16},{16,8},{24,0},{1,25},{9,17},{17,9},{25,1},{2,26},{10... | collective-permute-start | bytes 368648 | tf_op jit(solution)/shard_map/ppermute | solution.py:125
  77.3 0.5 collective-permute-start.29
  77.8 5.8 %collective-permute-done.26.refs_2_ = bf16[32,8192]{1,0:T(8,128)(2,1)S(1)} collective-permute-done((bf16[32,8192]{1,0:T(8,128)(2,1)}, bf16[32,8192]{1,0:T(8,128)(2,1)S(1)}, u32[]{:S(2)}, u32[]{:S(2)}) %collective-permute-start.26) | collective-permute-done | bytes 524320 | tf_op jit(solution)/shard_map/ppermute | solution.py:125
  83.6 0.6 collective-permute-start.27
  84.2 10.6 %collective-permute-done.30.refs_6_ = bf16[32,8192]{1,0:T(8,128)(2,1)S(1)} collective-permute-done((bf16[32,8192]{1,0:T(8,128)(2,1)S(1)}, bf16[32,8192]{1,0:T(8,128)(2,1)S(1)}, u32[]{:S(2)}, u32[]{:S(2)}) %collective-permute-start.30) | collective-permute-done | bytes 524320 | tf_op jit(solution)/shard_map/ppermute | solution.py:125
  94.8 0.1 collective-permute-start.31
  94.9 4.2 %collective-permute-start.21 = (bf16[16,3840]{1,0:T(8,128)(2,1)S(1)}, bf16[16,3840]{1,0:T(8,128)(2,1)S(1)}, u32[]{:S(2)}, u32[]{:S(2)}) collective-permute-start(bf16[16,3840]{1,0:T(8,128)(2,1)S(1)} %maximum_maximum_fusion.refs_0_), channel_id=1, source_target_pairs={{0,16},{8,24},{16,0},{24,8},{1,17},{9,25},{17,1},{25,9},{2,18},{10... | collective-permute-start | bytes 368648 | tf_op jit(solution)/shard_map/ppermute | solution.py:125
  99.2 6.6 %collective-permute-done.21.refs_2_ = bf16[16,3840]{1,0:T(8,128)(2,1)S(1)} collective-permute-done((bf16[16,3840]{1,0:T(8,128)(2,1)S(1)}, bf16[16,3840]{1,0:T(8,128)(2,1)S(1)}, u32[]{:S(2)}, u32[]{:S(2)}) %collective-permute-start.21) | collective-permute-done | bytes 122912 | tf_op jit(solution)/shard_map/ppermute | solution.py:125
  105.8 5.2 %collective-permute-done.20.refs_1_ = bf16[16,3840]{1,0:T(8,128)(2,1)S(1)} collective-permute-done((bf16[16,3840]{1,0:T(8,128)(2,1)S(1)}, bf16[16,3840]{1,0:T(8,128)(2,1)S(1)}, u32[]{:S(2)}, u32[]{:S(2)}) %collective-permute-start.20) | collective-permute-done | bytes 122912 | tf_op jit(solution)/shard_map/ppermute | solution.py:125
  110.9 0.7 join.1
  111.7 0.7 collective-permute-start.23
  112.4 0.1 stack.47.place
  112.5 6.8 %collective-permute-done.23.refs_0_ = bf16[64,2048]{1,0:T(8,128)(2,1)} collective-permute-done((bf16[64,2048]{1,0:T(8,128)(2,1)}, bf16[64,2048]{1,0:T(8,128)(2,1)}, u32[]{:S(2)}, u32[]{:S(2)}) %collective-permute-start.23) | collective-permute-done | bytes 262176 | tf_op jit(solution)/shard_map/ppermute | solution.py:125
  119.3 1.0 copy-done.4
  120.3 15.7 %early.1 = (f32[1792,256]{1,0:T(8,128)S(1)}, bf16[256,8192]{1,0:T(8,128)(2,1)S(1)}) custom-call(s32[8]{0:T(128)S(1)} %stack.47.place, bf16[32,8192]{1,0:T(8,128)(2,1)S(1)} %copy-done.4, bf16[32,8192]{1,0:T(8,128)(2,1)S(1)} %collective-permute-done.25.refs_1_, bf16[32,8192]{1,0:T(8,128)(2,1)S(1)} %collective-permute-done.26.refs_2_, ...), custom_call_target="tpu_custom_call" | custom-call | flops 7516192768 | bytes 37748736 | tf_op jit(solution)/shard_map/early/pallas_call | solution.py:386
  136.1 12.7 %merge0.1 = (bf16[1792,8192]{1,0:T(8,128)(2,1)}, f32[64,256]{1,0:T(8,128)S(1)}) custom-call(s32[1]{0:T(128)} %bitcast.16.slot, bf16[64,2048]{1,0:T(8,128)(2,1)} %get-tuple-element.54.refs_0_, bf16[64,1792]{1,0:T(8,128)(2,1)S(1)} %get-tuple-element.55.refs_1_, bf16[1792,8192]{1,0:T(8,128)(2,1)} %refs_2_.7, bf16[256,8192]{1,0:T(8,128)(2,1)S(1)} %get-tuple-element.56.refs_3_), custom_call_target="tpu_custom_call" | custom-call | flops 469762048 | bytes 14680064 | tf_op jit(solution)/shard_map/merge0/pallas_call | solution.py:436
  148.8 10.5 %merge1.1 = (bf16[1792,8192]{1,0:T(8,128)(2,1)}, f32[64,256]{1,0:T(8,128)S(1)}) custom-call(s32[1]{0:T(128)} %bitcast.15.slot, bf16[64,2048]{1,0:T(8,128)(2,1)S(1)} %collective-permute-done.32.refs_0_, bf16[64,1792]{1,0:T(8,128)(2,1)S(1)} %get-tuple-element.55.refs_1_, bf16[1792,8192]{1,0:T(8,128)(2,1)} %refs_2_.7, ...), custom_call_target="tpu_custom_call", output_to_operand_aliasing={{0}: (5, {})} | custom-call | flops 469762048 | bytes 14680064 | tf_op jit(solution)/shard_map/merge1/pallas_call | solution.py:436
  159.3 10.6 %merge2.1 = (bf16[1792,8192]{1,0:T(8,128)(2,1)}, f32[64,256]{1,0:T(8,128)S(1)}) custom-call(s32[1]{0:T(128)} %bitcast.14.slot, bf16[64,2048]{1,0:T(8,128)(2,1)} %collective-permute-done.23.refs_0_, bf16[64,1792]{1,0:T(8,128)(2,1)S(1)} %get-tuple-element.55.refs_1_, bf16[1792,8192]{1,0:T(8,128)(2,1)} %refs_2_.7, ...), custom_call_target="tpu_custom_call", output_to_operand_aliasing={{0}: (5, {})} | custom-call | flops 469762048 | bytes 14680064 | tf_op jit(solution)/shard_map/merge2/pallas_call | solution.py:436
  169.9 10.8 %merge3.1 = (bf16[1792,8192]{1,0:T(8,128)(2,1)}, f32[64,256]{1,0:T(8,128)}, bf16[1792,256]{1,0:T(8,128)(2,1)}) custom-call(s32[1]{0:T(128)} %bitcast.1.slot, bf16[64,2048]{1,0:T(8,128)(2,1)S(1)} %collective-permute-done.24.refs_0_, bf16[64,1792]{1,0:T(8,128)(2,1)S(1)} %get-tuple-element.55.refs_1_, ...), custom_call_target="tpu_custom_call", output_to_operand_aliasing={{0}: (5, {})} | custom-call | flops 469762048 | bytes 14680064 | tf_op jit(solution)/shard_map/merge3/pallas_call | solution.py:436
  (39 shorter events, 0.2 us)
Async XLA Ops:
  2.4 11.4 %collective-permute-start.6 = (bf16[8,5632]{1,0:T(8,128)(2,1)S(1)}, bf16[8,5632]{1,0:T(8,128)(2,1)S(1)}, u32[]{:S(2)}, u32[]{:S(2)}) collective-permute-start(bf16[8,5632]{1,0:T(8,128)(2,1)S(1)} %pad_maximum_fusion.refs_0_), channel_id=1, source_target_pairs={{0,28},{4,24},{8,20},{12,16},{16,12},{20,8},{24,4},{28,0},{1,29},{... | collective-permute-start | bytes 270344 | tf_op jit(solution)/shard_map/ppermute | solution.py:125
  8.5 10.3 %collective-permute-start.5 = (bf16[8,5632]{1,0:T(8,128)(2,1)S(1)}, bf16[8,5632]{1,0:T(8,128)(2,1)S(1)}, u32[]{:S(2)}, u32[]{:S(2)}) collective-permute-start(bf16[8,5632]{1,0:T(8,128)(2,1)S(1)} %pad_maximum_fusion.refs_0_), channel_id=1, source_target_pairs={{0,24},{4,28},{8,16},{12,20},{16,8},{20,12},{24,0},{28,4},{1,25},{... | collective-permute-start | bytes 270344 | tf_op jit(solution)/shard_map/ppermute | solution.py:125
  8.7 14.2 %collective-permute-start.4 = (bf16[8,5632]{1,0:T(8,128)(2,1)S(1)}, bf16[8,5632]{1,0:T(8,128)(2,1)S(1)}, u32[]{:S(2)}, u32[]{:S(2)}) collective-permute-start(bf16[8,5632]{1,0:T(8,128)(2,1)S(1)} %pad_maximum_fusion.refs_0_), channel_id=1, source_target_pairs={{0,20},{4,16},{8,28},{12,24},{16,4},{20,0},{24,12},{28,8},{1,21},{... | collective-permute-start | bytes 270344 | tf_op jit(solution)/shard_map/ppermute | solution.py:125
  9.5 14.4 %collective-permute-start.3 = (bf16[8,5632]{1,0:T(8,128)(2,1)S(1)}, bf16[8,5632]{1,0:T(8,128)(2,1)S(1)}, u32[]{:S(2)}, u32[]{:S(2)}) collective-permute-start(bf16[8,5632]{1,0:T(8,128)(2,1)S(1)} %pad_maximum_fusion.refs_0_), channel_id=1, source_target_pairs={{0,16},{4,20},{8,24},{12,28},{16,0},{20,4},{24,8},{28,12},{1,17},{... | collective-permute-start | bytes 270344 | tf_op jit(solution)/shard_map/ppermute | solution.py:125
  11.5 12.4 %collective-permute-start.2 = (bf16[8,5632]{1,0:T(8,128)(2,1)S(1)}, bf16[8,5632]{1,0:T(8,128)(2,1)S(1)}, u32[]{:S(2)}, u32[]{:S(2)}) collective-permute-start(bf16[8,5632]{1,0:T(8,128)(2,1)S(1)} %pad_maximum_fusion.refs_0_), channel_id=1, source_target_pairs={{0,12},{4,8},{8,4},{12,0},{16,28},{20,24},{24,20},{28,16},{1,13},{... | collective-permute-start | bytes 270344 | tf_op jit(solution)/shard_map/ppermute | solution.py:125
  13.8 10.7 %collective-permute-start.1 = (bf16[8,5632]{1,0:T(8,128)(2,1)S(1)}, bf16[8,5632]{1,0:T(8,128)(2,1)S(1)}, u32[]{:S(2)}, u32[]{:S(2)}) collective-permute-start(bf16[8,5632]{1,0:T(8,128)(2,1)S(1)} %pad_maximum_fusion.refs_0_), channel_id=1, source_target_pairs={{0,8},{4,12},{8,0},{12,4},{16,24},{20,28},{24,16},{28,20},{1,9},{5... | collective-permute-start | bytes 270344 | tf_op jit(solution)/shard_map/ppermute | solution.py:125
  18.8 5.7 %collective-permute-start = (bf16[8,5632]{1,0:T(8,128)(2,1)S(1)}, bf16[8,5632]{1,0:T(8,128)(2,1)S(1)}, u32[]{:S(2)}, u32[]{:S(2)}) collective-permute-start(bf16[8,5632]{1,0:T(8,128)(2,1)S(1)} %pad_maximum_fusion.refs_0_), channel_id=1, source_target_pairs={{0,4},{4,0},{8,12},{12,8},{16,20},{20,16},{24,28},{28,24},{1,5},{5... | collective-permute-start | bytes 270344 | tf_op jit(solution)/shard_map/ppermute | solution.py:125
  24.5 1.5 copy-start
  26.0 1.2 copy-start.2
  28.2 5.8 %collective-permute-start.9 = (f32[128,256]{1,0:T(8,128)S(1)}, f32[128,256]{1,0:T(8,128)S(1)}, u32[]{:S(2)}, u32[]{:S(2)}) collective-permute-start(f32[128,256]{1,0:T(8,128)S(1)} %low.1.refs_0_), channel_id=1, source_target_pairs={{0,3},{1,2},{2,1},{3,0},{4,7},{5,6},{6,5},{7,4},{8,11},{9,10},{10,... | collective-permute-start | bytes 393224 | tf_op jit(solution)/shard_map/ppermute | solution.py:125
  28.3 8.6 %collective-permute-start.8 = (f32[128,256]{1,0:T(8,128)S(1)}, f32[128,256]{1,0:T(8,128)S(1)}, u32[]{:S(2)}, u32[]{:S(2)}) collective-permute-start(f32[128,256]{1,0:T(8,128)S(1)} %low.1.refs_0_), channel_id=1, source_target_pairs={{0,2},{1,3},{2,0},{3,1},{4,6},{5,7},{6,4},{7,5},{8,10},{9,11},{10,... | collective-permute-start | bytes 393224 | tf_op jit(solution)/shard_map/ppermute | solution.py:125
  29.9 7.0 %collective-permute-start.7 = (f32[128,256]{1,0:T(8,128)S(1)}, f32[128,256]{1,0:T(8,128)S(1)}, u32[]{:S(2)}, u32[]{:S(2)}) collective-permute-start(f32[128,256]{1,0:T(8,128)S(1)} %low.1.refs_0_), channel_id=1, source_target_pairs={{0,1},{1,0},{2,3},{3,2},{4,5},{5,4},{6,7},{7,6},{8,9},{9,8},{10,11... | collective-permute-start | bytes 393224 | tf_op jit(solution)/shard_map/ppermute | solution.py:125
  30.1 40.8 %collective-permute-start.28 = (bf16[32,8192]{1,0:T(8,128)(2,1)}, bf16[32,8192]{1,0:T(8,128)(2,1)S(1)}, u32[]{:S(2)}, u32[]{:S(2)}) collective-permute-start(bf16[32,8192]{1,0:T(8,128)(2,1)} %refs_0_.1), channel_id=1, source_target_pairs={{0,4},{4,0},{1,5},{5,1},{2,6},{6,2},{3,7},{7,3},{8,12},{12,8},{9,1... | collective-permute-start | bytes 1572872 | tf_op jit(solution)/shard_map/ppermute | solution.py:125
  36.9 1.5 copy-start.1
  38.4 1.2 copy-start.3
  40.2 6.9 %collective-permute-start.10 = (bf16[8,5632]{1,0:T(8,128)(2,1)S(1)}, bf16[8,5632]{1,0:T(8,128)(2,1)S(1)}, u32[]{:S(2)}, u32[]{:S(2)}) collective-permute-start(bf16[8,5632]{1,0:T(8,128)(2,1)S(1)} %get-tuple-element.38), channel_id=1, source_target_pairs={{0,4},{4,0},{8,12},{12,8},{16,20},{20,16},{24,28},{28,24},{1,5},{5... | collective-permute-start | bytes 270344 | tf_op jit(solution)/shard_map/ppermute | solution.py:125
  41.1 8.8 %collective-permute-start.11 = (bf16[8,5632]{1,0:T(8,128)(2,1)S(1)}, bf16[8,5632]{1,0:T(8,128)(2,1)S(1)}, u32[]{:S(2)}, u32[]{:S(2)}) collective-permute-start(bf16[8,5632]{1,0:T(8,128)(2,1)S(1)} %get-tuple-element.39), channel_id=1, source_target_pairs={{0,8},{4,12},{8,0},{12,4},{16,24},{20,28},{24,16},{28,20},{1,9},{5... | collective-permute-start | bytes 270344 | tf_op jit(solution)/shard_map/ppermute | solution.py:125
  42.3 8.8 %collective-permute-start.12 = (bf16[8,5632]{1,0:T(8,128)(2,1)S(1)}, bf16[8,5632]{1,0:T(8,128)(2,1)S(1)}, u32[]{:S(2)}, u32[]{:S(2)}) collective-permute-start(bf16[8,5632]{1,0:T(8,128)(2,1)S(1)} %get-tuple-element.40), channel_id=1, source_target_pairs={{0,12},{4,8},{8,4},{12,0},{16,28},{20,24},{24,20},{28,16},{1,13},{... | collective-permute-start | bytes 270344 | tf_op jit(solution)/shard_map/ppermute | solution.py:125
  43.8 11.0 %collective-permute-start.13 = (bf16[8,5632]{1,0:T(8,128)(2,1)S(1)}, bf16[8,5632]{1,0:T(8,128)(2,1)S(1)}, u32[]{:S(2)}, u32[]{:S(2)}) collective-permute-start(bf16[8,5632]{1,0:T(8,128)(2,1)S(1)} %get-tuple-element.41), channel_id=1, source_target_pairs={{0,16},{4,20},{8,24},{12,28},{16,0},{20,4},{24,8},{28,12},{1,17},{... | collective-permute-start | bytes 270344 | tf_op jit(solution)/shard_map/ppermute | solution.py:125
  47.1 12.7 %collective-permute-start.14 = (bf16[8,5632]{1,0:T(8,128)(2,1)S(1)}, bf16[8,5632]{1,0:T(8,128)(2,1)S(1)}, u32[]{:S(2)}, u32[]{:S(2)}) collective-permute-start(bf16[8,5632]{1,0:T(8,128)(2,1)S(1)} %get-tuple-element.42), channel_id=1, source_target_pairs={{0,20},{4,16},{8,28},{12,24},{16,4},{20,0},{24,12},{28,8},{1,21},{... | collective-permute-start | bytes 270344 | tf_op jit(solution)/shard_map/ppermute | solution.py:125
  49.9 9.9 %collective-permute-start.15 = (bf16[8,5632]{1,0:T(8,128)(2,1)S(1)}, bf16[8,5632]{1,0:T(8,128)(2,1)S(1)}, u32[]{:S(2)}, u32[]{:S(2)}) collective-permute-start(bf16[8,5632]{1,0:T(8,128)(2,1)S(1)} %get-tuple-element.43), channel_id=1, source_target_pairs={{0,24},{4,28},{8,16},{12,20},{16,8},{20,12},{24,0},{28,4},{1,25},{... | collective-permute-start | bytes 270344 | tf_op jit(solution)/shard_map/ppermute | solution.py:125
  51.1 8.7 %collective-permute-start.16 = (bf16[8,5632]{1,0:T(8,128)(2,1)S(1)}, bf16[8,5632]{1,0:T(8,128)(2,1)S(1)}, u32[]{:S(2)}, u32[]{:S(2)}) collective-permute-start(bf16[8,5632]{1,0:T(8,128)(2,1)S(1)} %get-tuple-element.44), channel_id=1, source_target_pairs={{0,28},{4,24},{8,20},{12,16},{16,12},{20,8},{24,4},{28,0},{1,29},{... | collective-permute-start | bytes 270344 | tf_op jit(solution)/shard_map/ppermute | solution.py:125
  59.8 0.9 copy-start.5
  60.7 0.8 copy-start.6
  61.6 0.9 copy-start.7
  62.5 0.9 copy-start.8
  63.4 0.8 copy-start.9
  64.2 0.8 copy-start.10
  66.0 4.8 %collective-permute-start.17 = (bf16[8,1792]{1,0:T(8,128)(2,1)S(1)}, bf16[8,1792]{1,0:T(8,128)(2,1)S(1)}, u32[]{:S(2)}, u32[]{:S(2)}) collective-permute-start(bf16[8,1792]{1,0:T(8,128)(2,1)S(1)} %get-tuple-element.52), channel_id=1, source_target_pairs={{0,0},{1,2},{2,4},{3,6},{4,1},{5,3},{6,5},{7,7},{8,8},{9,10},{10,1... | collective-permute-start | bytes 86024 | tf_op jit(solution)/shard_map/ppermute | solution.py:326
  66.7 4.2 %collective-permute-start.18 = (bf16[8,1792]{1,0:T(8,128)(2,1)S(1)}, bf16[8,1792]{1,0:T(8,128)(2,1)S(1)}, u32[]{:S(2)}, u32[]{:S(2)}) collective-permute-start(bf16[8,1792]{1,0:T(8,128)(2,1)S(1)} %get-tuple-element.53), channel_id=1, source_target_pairs={{0,1},{1,3},{2,5},{3,7},{4,0},{5,2},{6,4},{7,6},{8,9},{9,11},{10,1... | collective-permute-start | bytes 86024 | tf_op jit(solution)/shard_map/ppermute | solution.py:326
  68.8 14.7 %collective-permute-start.26 = (bf16[32,8192]{1,0:T(8,128)(2,1)}, bf16[32,8192]{1,0:T(8,128)(2,1)S(1)}, u32[]{:S(2)}, u32[]{:S(2)}) collective-permute-start(bf16[32,8192]{1,0:T(8,128)(2,1)} %refs_0_.1), channel_id=1, source_target_pairs={{0,2},{1,3},{2,0},{3,1},{4,6},{5,7},{6,4},{7,5},{8,10},{9,11},{10,... | collective-permute-start | bytes 1572872 | tf_op jit(solution)/shard_map/ppermute | solution.py:125
  70.3 4.3 %collective-permute-start.19 = (bf16[8,2048]{1,0:T(8,128)(2,1)S(1)}, bf16[8,2048]{1,0:T(8,128)(2,1)S(1)}, u32[]{:S(2)}, u32[]{:S(2)}) collective-permute-start(bf16[8,2048]{1,0:T(8,128)(2,1)S(1)} %get-tuple-element.51), channel_id=1, source_target_pairs={{0,4},{4,0},{1,5},{5,1},{2,6},{6,2},{3,7},{7,3},{8,12},{12,8},{9,1... | collective-permute-start | bytes 98312 | tf_op jit(solution)/shard_map/ppermute | solution.py:125
  70.9 23.9 %collective-permute-start.30 = (bf16[32,8192]{1,0:T(8,128)(2,1)S(1)}, bf16[32,8192]{1,0:T(8,128)(2,1)S(1)}, u32[]{:S(2)}, u32[]{:S(2)}) collective-permute-start(bf16[32,8192]{1,0:T(8,128)(2,1)S(1)} %collective-permute-done.28.refs_4_), channel_id=1, source_target_pairs={{0,2},{1,3},{2,0},{3,1},{4,6},{5,7},{6,4},{7,5},{8,10},{9,11},{10,... | collective-permute-start | bytes 1572872 | tf_op jit(solution)/shard_map/ppermute | solution.py:125
  74.6 20.3 %collective-permute-start.22 = (bf16[16,3840]{1,0:T(8,128)(2,1)S(1)}, bf16[16,3840]{1,0:T(8,128)(2,1)S(1)}, u32[]{:S(2)}, u32[]{:S(2)}) collective-permute-start(bf16[16,3840]{1,0:T(8,128)(2,1)S(1)} %maximum_maximum_fusion.refs_0_), channel_id=1, source_target_pairs={{0,24},{8,16},{16,8},{24,0},{1,25},{9,17},{17,9},{25,1},{2,26},{10... | collective-permute-start | bytes 368648 | tf_op jit(solution)/shard_map/ppermute | solution.py:125
  77.3 35.1 %collective-permute-start.25 = (bf16[32,8192]{1,0:T(8,128)(2,1)}, bf16[32,8192]{1,0:T(8,128)(2,1)S(1)}, u32[]{:S(2)}, u32[]{:S(2)}) collective-permute-start(bf16[32,8192]{1,0:T(8,128)(2,1)} %refs_0_.1), channel_id=1, source_target_pairs={{0,1},{1,0},{2,3},{3,2},{4,5},{5,4},{6,7},{7,6},{8,9},{9,8},{10,11... | collective-permute-start | bytes 1572872 | tf_op jit(solution)/shard_map/ppermute | solution.py:125
  77.3 42.0 %collective-permute-start.29 = (bf16[32,8192]{1,0:T(8,128)(2,1)S(1)}, bf16[32,8192]{1,0:T(8,128)(2,1)S(1)}, u32[]{:S(2)}, u32[]{:S(2)}) collective-permute-start(bf16[32,8192]{1,0:T(8,128)(2,1)S(1)} %collective-permute-done.28.refs_4_), channel_id=1, source_target_pairs={{0,1},{1,0},{2,3},{3,2},{4,5},{5,4},{6,7},{7,6},{8,9},{9,8},{10,11... | collective-permute-start | bytes 1572872 | tf_op jit(solution)/shard_map/ppermute | solution.py:125
  83.6 35.7 %collective-permute-start.27 = (bf16[32,8192]{1,0:T(8,128)(2,1)S(1)}, bf16[32,8192]{1,0:T(8,128)(2,1)S(1)}, u32[]{:S(2)}, u32[]{:S(2)}) collective-permute-start(bf16[32,8192]{1,0:T(8,128)(2,1)S(1)} %collective-permute-done.26.refs_2_), channel_id=1, source_target_pairs={{0,1},{1,0},{2,3},{3,2},{4,5},{5,4},{6,7},{7,6},{8,9},{9,8},{10,11... | collective-permute-start | bytes 1572872 | tf_op jit(solution)/shard_map/ppermute | solution.py:125
  94.8 24.5 %collective-permute-start.31 = (bf16[32,8192]{1,0:T(8,128)(2,1)S(1)}, bf16[32,8192]{1,0:T(8,128)(2,1)}, u32[]{:S(2)}, u32[]{:S(2)}) collective-permute-start(bf16[32,8192]{1,0:T(8,128)(2,1)S(1)} %collective-permute-done.30.refs_6_), channel_id=1, source_target_pairs={{0,1},{1,0},{2,3},{3,2},{4,5},{5,4},{6,7},{7,6},{8,9},{9,8},{10,11... | collective-permute-start | bytes 1572872 | tf_op jit(solution)/shard_map/ppermute | solution.py:125
  94.9 10.8 %collective-permute-start.21 = (bf16[16,3840]{1,0:T(8,128)(2,1)S(1)}, bf16[16,3840]{1,0:T(8,128)(2,1)S(1)}, u32[]{:S(2)}, u32[]{:S(2)}) collective-permute-start(bf16[16,3840]{1,0:T(8,128)(2,1)S(1)} %maximum_maximum_fusion.refs_0_), channel_id=1, source_target_pairs={{0,16},{8,24},{16,0},{24,8},{1,17},{9,25},{17,1},{25,9},{2,18},{10... | collective-permute-start | bytes 368648 | tf_op jit(solution)/shard_map/ppermute | solution.py:125
  105.8 5.2 %collective-permute-start.20 = (bf16[16,3840]{1,0:T(8,128)(2,1)S(1)}, bf16[16,3840]{1,0:T(8,128)(2,1)S(1)}, u32[]{:S(2)}, u32[]{:S(2)}) collective-permute-start(bf16[16,3840]{1,0:T(8,128)(2,1)S(1)} %maximum_maximum_fusion.refs_0_), channel_id=1, source_target_pairs={{0,8},{8,0},{16,24},{24,16},{1,9},{9,1},{17,25},{25,17},{2,10},{10... | collective-permute-start | bytes 368648 | tf_op jit(solution)/shard_map/ppermute | solution.py:125
  111.7 7.6 %collective-permute-start.23 = (bf16[64,2048]{1,0:T(8,128)(2,1)}, bf16[64,2048]{1,0:T(8,128)(2,1)}, u32[]{:S(2)}, u32[]{:S(2)}) collective-permute-start(bf16[64,2048]{1,0:T(8,128)(2,1)} %get-tuple-element.54.refs_0_), channel_id=1, source_target_pairs={{0,2},{1,3},{2,0},{3,1},{4,6},{5,7},{6,4},{7,5},{8,10},{9,11},{10,... | collective-permute-start | bytes 786440 | tf_op jit(solution)/shard_map/ppermute | solution.py:125
  112.5 36.4 %collective-permute-start.32 = (bf16[64,2048]{1,0:T(8,128)(2,1)}, bf16[64,2048]{1,0:T(8,128)(2,1)S(1)}, u32[]{:S(2)}, u32[]{:S(2)}) collective-permute-start(bf16[64,2048]{1,0:T(8,128)(2,1)} %get-tuple-element.54.refs_0_), channel_id=1, source_target_pairs={{0,1},{1,0},{2,3},{3,2},{4,5},{5,4},{6,7},{7,6},{8,9},{9,8},{10,11... | collective-permute-start | bytes 786440 | tf_op jit(solution)/shard_map/ppermute | solution.py:125
  119.3 50.6 %collective-permute-start.24 = (bf16[64,2048]{1,0:T(8,128)(2,1)}, bf16[64,2048]{1,0:T(8,128)(2,1)S(1)}, u32[]{:S(2)}, u32[]{:S(2)}) collective-permute-start(bf16[64,2048]{1,0:T(8,128)(2,1)} %collective-permute-done.23.refs_0_), channel_id=1, source_target_pairs={{0,1},{1,0},{2,3},{3,2},{4,5},{5,4},{6,7},{7,6},{8,9},{9,8},{10,11... | collective-permute-start | bytes 786440 | tf_op jit(solution)/shard_map/ppermute | solution.py:125
  119.3 1.0 copy-start.4
